TPU v7x, 32 devices: a whole 2x2x4 slice. The times are simulated.
32 devices in a mesh: group: 2 (over y), expert: 4 (over z), tensor: 4 (over x, core).
Axes of the slice: x: 2, y: 2, z: 4, core: 2. Of those that a mesh axis runs over, the one named last changes fastest.
Arguments:
- tokens: bfloat16 [2048, 4096], P(('group', 'expert', 'tensor')), parts along dimension 0, may hold values from -6 to 6
- cotangent: bfloat16 [2048, 4096], P(('group', 'expert', 'tensor')), parts along dimension 0, may hold values from -6 to 6
- expert_ids: int32 [2048, 2], P(('group', 'expert', 'tensor')), parts along dimension 0, may hold values from 0 to 3, all different within a row
- gate_wts: float32 [2048, 2], P(('group', 'expert', 'tensor')), parts along dimension 0, may hold values from 0.2 to 1
- w_gate: bfloat16 [4, 4096, 256], P('expert', 'tensor'), may hold values from -0.09375 to 0.09375
- w_up: bfloat16 [4, 4096, 256], P('expert', 'tensor'), may hold values from -0.09375 to 0.09375
- w_down: bfloat16 [4, 256, 4096], P('expert', 'tensor'), may hold values from -0.375 to 0.375
Outputs:
- input_grad: bfloat16 [2048, 4096], P(('group', 'expert', 'tensor')), parts along dimension 0
- grad_gate: bfloat16 [8, 4096, 256], P(('group', 'expert'), 'tensor'), parts along dimension 0
- grad_up: bfloat16 [8, 4096, 256], P(('group', 'expert'), 'tensor'), parts along dimension 0
- grad_down: bfloat16 [8, 256, 4096], P(('group', 'expert'), 'tensor'), parts along dimension 0
There are 2 independent parts, one for each index of `group`. A program takes and returns all parts, laid end to end along the dimension named above; an argument that names none is the same for every part. Nothing has to cross between parts.
Inputs may be any that keep to these rules, and one draw needn't show every extreme that they name: `expert_ids`: the two ids of a token differ.
All inputs are finite; a program needn't handle non-finite values.
Results may differ from a plain program's by a relative error of at most 0.009.
Values may be sent and summed in bfloat16 or wider, within the bound.
A program may use at most 64 MiB of HBM per device.

v0:
```python
import jax
import jax.numpy as jnp
from jax import lax
from jax.sharding import PartitionSpec as P


def contract_last(left, right):
    return lax.dot_general(
        left, right, (((1,), (1,)), ((), ())), preferred_element_type=jnp.float32
    )


def contract_first(left, right):
    return lax.dot_general(
        left, right, (((0,), (0,)), ((), ())), preferred_element_type=jnp.float32
    )


def local(tokens, cotangent, expert_ids, gate_wts, w_gate, w_up, w_down):
    tok_rows, model_width = tokens.shape
    experts = lax.axis_size("expert")
    capacity = 2 * tok_rows // experts
    slots_all = experts * capacity
    zero_half = jnp.zeros((), jnp.bfloat16)
    flat_ids = expert_ids.reshape(-1)
    onehot = (flat_ids[:, None] == jnp.arange(experts, dtype=jnp.int32)[None, :]).astype(jnp.int32)
    positions = jnp.sum(onehot * (jnp.cumsum(onehot, axis=0) - 1), axis=1)
    retained = positions < capacity
    target = jnp.where(retained, flat_ids * capacity + positions, slots_all)
    anchor = (
        jnp.full((slots_all,), -1, jnp.int32)
        .at[target]
        .set(jnp.arange(2 * tok_rows, dtype=jnp.int32), mode="drop")
    )
    populated_rows = anchor >= 0
    picked = jnp.maximum(anchor, 0)
    tok_index = picked // 2
    send_rows = jnp.where(populated_rows[:, None], tokens[tok_index], zero_half)
    gate_scale = gate_wts.reshape(-1)[picked]
    scaled = (gate_scale[:, None] * cotangent[tok_index].astype(jnp.float32)).astype(jnp.bfloat16)
    send_cot = jnp.where(populated_rows[:, None], scaled, zero_half)
    recv_rows, recv_cot = (
        lax.all_to_all(
            send_rows.reshape(experts, capacity, model_width),
            "expert",
            split_axis=0,
            concat_axis=0,
            tiled=True,
        ),
        lax.all_to_all(
            send_cot.reshape(experts, capacity, model_width),
            "expert",
            split_axis=0,
            concat_axis=0,
            tiled=True,
        ),
    )
    rows_in = recv_rows.reshape(slots_all, model_width)
    cot_in = recv_cot.reshape(slots_all, model_width)
    gate_shard = w_gate[0]
    up_shard = w_up[0]
    down_shard = w_down[0]
    hidden_width = gate_shard.shape[1]
    full_gate, full_up, complete_down_weight = (
        lax.all_gather(gate_shard, "tensor", axis=0, tiled=True),
        lax.all_gather(up_shard, "tensor", axis=0, tiled=True),
        lax.all_gather(down_shard, "tensor", axis=0, tiled=True),
    )
    pre_gate = jnp.dot(rows_in, full_gate, preferred_element_type=jnp.float32)
    pre_up = jnp.dot(rows_in, full_up, preferred_element_type=jnp.float32)
    grad_hidden = contract_last(cot_in, complete_down_weight)
    sigmoid_gate = jax.nn.sigmoid(pre_gate)
    activated = pre_gate * sigmoid_gate
    hidden = (activated * pre_up).astype(jnp.bfloat16)
    grad_gate_pre = (
        grad_hidden * pre_up * sigmoid_gate * (1.0 + pre_gate * (1.0 - sigmoid_gate))
    ).astype(jnp.bfloat16)
    grad_up_pre = (grad_hidden * activated).astype(jnp.bfloat16)
    joint_grad = jnp.concatenate([grad_gate_pre, grad_up_pre], axis=1)
    columns = rows_in
    summed = lax.psum_scatter(
        contract_first(columns, joint_grad).astype(jnp.bfloat16),
        "tensor",
        scatter_dimension=0,
        tiled=True,
    ).astype(jnp.float32)
    columns = hidden
    summed_down = lax.psum_scatter(
        contract_first(columns, cot_in).astype(jnp.bfloat16),
        "tensor",
        scatter_dimension=0,
        tiled=True,
    )
    rows_out = (
        contract_last(grad_gate_pre, full_gate) + contract_last(grad_up_pre, full_up)
    ).astype(jnp.bfloat16)
    returned = lax.all_to_all(
        rows_out.reshape(experts, capacity, model_width),
        "expert",
        split_axis=0,
        concat_axis=0,
        tiled=True,
    )
    returned = returned.reshape(slots_all, model_width)
    gathered = returned[jnp.minimum(target, slots_all - 1)].astype(jnp.float32)
    gathered = jnp.where(retained[:, None], gathered, jnp.zeros((), jnp.float32))
    input_grad = jnp.sum(gathered.reshape(tok_rows, 2, model_width), axis=1).astype(jnp.bfloat16)
    return (
        input_grad,
        summed[:, :hidden_width].astype(jnp.bfloat16)[None],
        summed[:, hidden_width:].astype(jnp.bfloat16)[None],
        summed_down[None],
    )


def solution(mesh):
    return jax.shard_map(
        local,
        mesh=mesh,
        in_specs=(
            P(("group", "expert", "tensor"), None),
            P(("group", "expert", "tensor"), None),
            P(("group", "expert", "tensor"), None),
            P(("group", "expert", "tensor"), None),
            P("expert", "tensor", None),
            P("expert", "tensor", None),
            P("expert", "tensor", None),
        ),
        out_specs=(
            P(("group", "expert", "tensor"), None),
            P(("group", "expert"), "tensor", None),
            P(("group", "expert"), "tensor", None),
            P(("group", "expert"), "tensor", None),
        ),
        check_vma=False,
    )
```

profile of v0, /device:TPU:0, one launch (start us, length us, event | category | flops | bytes accessed | tf_op | source)
XLA Modules:
  0.0 174.4 jit_solution(17855843057683153591)
XLA Ops:
  7.2 0.0 copy-start
  7.2 0.0 all-gather.11.cloned.1.call-start
  7.2 0.7 all-gather.11.cloned.1.call-update
  7.9 0.0 all-gather.9.cloned.1.call-start
  8.0 0.7 all-gather.9.cloned.1.call-update
  8.7 0.8 copy.14
  9.4 0.7 broadcast_multiply_fusion
  10.1 0.1 copy.15
  10.2 0.1 mul.54
  10.4 0.1 eq.15
  10.5 0.8 copy.16
  11.3 0.1 reshape.115
  11.4 0.1 fusion.16
  11.5 0.2 reduce_window_sum.11
  11.7 0.2 select_reduce_fusion.1
  11.9 1.0 scatter_custom_fusion
  12.9 1.2 gather_fusion
  14.1 0.1 mul.55
  14.2 0.1 broadcast_in_dim.63
  14.3 0.0 copy-done
  14.3 0.0 copy-start.1
  14.3 1.2 gather_fusion.1
  15.5 0.0 copy-done.1
  15.5 1.2 gather_fusion.2
  16.7 1.9 %fusion.11 = (bf16[4,32,4096]{2,1,0:T(8,128)(2,1)}, bf16[4,32,4096]{2,1,0:T(8,128)(2,1)}) fusion(bf16[4,32,4096]{2,1,0:T(8,128)(2,1)S(1)} %bitcast.53, f32[4,32]{1,0:T(4,128)S(1)} %mul.55, pred[4,32]{1,0:T(4,128)(4,1)S(1)} %broadcast_in_dim.63, bf16[4,32,4096]{2,1,0:T(8,128)(2,1)S(1)} %bitcast.54), kind=kLoop, calls=%fused_computation.21 | loop fusion | flops 2621440 | bytes 4194944 | tf_op jit(solution)/shard_map/jit(_where)/select_n | solution.py:41
  18.6 6.3 %all-to-all-start.1 = ((bf16[4,32,4096]{2,1,0:T(8,128)(2,1)}), bf16[4,32,4096]{2,1,0:T(8,128)(2,1)S(1)}, u32[]{:S(2)}, u32[]{:S(2)}) async-start(bf16[4,32,4096]{2,1,0:T(8,128)(2,1)} %get-tuple-element.11), calls=%async_computation.1 | async-start | bytes 2097152 | tf_op jit(solution)/shard_map/all_to_all | solution.py:43
  25.0 0.0 all-gather.7.cloned.1.call-start
  25.0 0.7 all-gather.7.cloned.1.call-update
  25.7 25.0 %all-to-all-done.1 = bf16[4,32,4096]{2,1,0:T(8,128)(2,1)S(1)} async-done(((bf16[4,32,4096]{2,1,0:T(8,128)(2,1)}), bf16[4,32,4096]{2,1,0:T(8,128)(2,1)S(1)}, u32[]{:S(2)}, u32[]{:S(2)}) %all-to-all-start.1) | async-done | bytes 1048608 | tf_op jit(solution)/shard_map/all_to_all | solution.py:43
  50.7 3.5 %all-to-all-start = ((bf16[4,32,4096]{2,1,0:T(8,128)(2,1)}), bf16[4,32,4096]{2,1,0:T(8,128)(2,1)S(1)}, u32[]{:S(2)}, u32[]{:S(2)}) async-start(bf16[4,32,4096]{2,1,0:T(8,128)(2,1)} %get-tuple-element.10), calls=%async_computation | async-start | bytes 2097152 | tf_op jit(solution)/shard_map/all_to_all | solution.py:50
  54.2 0.0 reduce-scatter.3.cloned.1.call-start
  54.3 0.0 all-gather.11.cloned.1.call-done
  54.3 2.0 %fusion.4 = f32[128,256]{1,0:T(8,128)S(1)} fusion(bf16[128,4096]{1,0:T(8,128)(2,1)S(1)} %bitcast.48, bf16[1,4096,256]{2,1,0:T(8,128)(2,1)} %all-gather.11.cloned.1.call-done), kind=kOutput, calls=%fused_computation.13 | convolution fusion | flops 268435456 | bytes 3276800 | tf_op jit(solution)/shard_map/dot_general | solution.py:69
  56.3 2.7 %all-gather.9.cloned.1.call-done = bf16[1,4096,256]{2,1,0:T(8,128)(2,1)} async-done(((bf16[1,1024,256]{2,1,0:T(8,128)(2,1)}), bf16[1,4096,256]{2,1,0:T(8,128)(2,1)}) %all-gather.9.cloned.1.call-update) | async-done | bytes 2097168 | tf_op jit(solution)/shard_map/all_gather | solution.py:66
  59.0 2.0 %fusion.7 = f32[128,256]{1,0:T(8,128)S(1)} fusion(bf16[128,4096]{1,0:T(8,128)(2,1)S(1)} %bitcast.49, bf16[1,4096,256]{2,1,0:T(8,128)(2,1)} %all-gather.9.cloned.1.call-done), kind=kOutput, calls=%fused_computation.16 | convolution fusion | flops 268435456 | bytes 3276800 | tf_op jit(solution)/shard_map/dot_general | solution.py:70
  61.1 18.4 %all-to-all-done = bf16[4,32,4096]{2,1,0:T(8,128)(2,1)S(1)} async-done(((bf16[4,32,4096]{2,1,0:T(8,128)(2,1)}), bf16[4,32,4096]{2,1,0:T(8,128)(2,1)S(1)}, u32[]{:S(2)}, u32[]{:S(2)}) %all-to-all-start) | async-done | bytes 1048608 | tf_op jit(solution)/shard_map/all_to_all | solution.py:50
  79.5 3.8 %all-gather.7.cloned.1.call-done = bf16[1,256,4096]{2,1,0:T(8,128)(2,1)} async-done(((bf16[1,64,4096]{2,1,0:T(8,128)(2,1)}), bf16[1,256,4096]{2,1,0:T(8,128)(2,1)}) %all-gather.7.cloned.1.call-update) | async-done | bytes 2097168 | tf_op jit(solution)/shard_map/all_gather | solution.py:67
  83.2 2.4 %multiply_convert_fusion.1 = (bf16[128,256]{1,0:T(8,128)(2,1)S(1)}, bf16[128,256]{1,0:T(8,128)(2,1)S(1)}) fusion(f32[128,256]{1,0:T(8,128)S(1)} %fusion.4, f32[128,256]{1,0:T(8,128)S(1)} %fusion.7, bf16[128,4096]{1,0:T(8,128)(2,1)S(1)} %bitcast.51, bf16[1,256,4096]{2,1,0:T(8,128)(2,1)} %all-gather.7.cloned.1.call-done), kind=kOutput, calls=%fused_computation.29 | convolution fusion | flops 268861440 | bytes 3538944 | tf_op jit(solution)/shard_map/dot_general | solution.py:8
  85.7 3.2 %convolution_convert_fusion = bf16[4096,512]{1,0:T(8,128)(2,1)} fusion(bf16[128,4096]{1,0:T(8,128)(2,1)S(1)} %bitcast.50, bf16[128,256]{1,0:T(8,128)(2,1)S(1)} %get-tuple-element.6, bf16[128,256]{1,0:T(8,128)(2,1)S(1)} %get-tuple-element.7), kind=kOutput, calls=%fused_computation.5 | convolution fusion | flops 539230208 | bytes 5373952 | tf_op jit(solution)/shard_map/dot_general | solution.py:14
  88.9 0.0 reduce-scatter.3.cloned.1.call-update
  88.9 0.0 reduce-scatter.5.cloned.1.call-start
  88.9 2.1 %convolution_convert_fusion.1 = bf16[256,4096]{1,0:T(8,128)(2,1)} fusion(bf16[128,4096]{1,0:T(8,128)(2,1)S(1)} %bitcast.52, f32[128,256]{1,0:T(8,128)S(1)} %fusion.7, f32[128,256]{1,0:T(8,128)S(1)} %fusion.4), kind=kOutput, calls=%fused_computation.6 | convolution fusion | flops 269680640 | bytes 3407872 | tf_op jit(solution)/shard_map/dot_general | solution.py:14
  91.1 0.0 copy-start.2
  91.1 0.0 reduce-scatter.5.cloned.1.call-update
  91.1 1.6 copy-done.2
  92.7 0.0 copy-start.3
  92.7 0.8 fusion.2
  93.5 0.8 copy-done.3
  94.3 1.8 %fusion = bf16[128,4096]{1,0:T(8,128)(2,1)} fusion(f32[128,4096]{1,0:T(8,128)S(1)} %fusion.2, bf16[128,256]{1,0:T(8,128)(2,1)S(1)} %get-tuple-element.6, bf16[1,4096,256]{2,1,0:T(8,128)(2,1)S(1)} %copy-done.3), kind=kOutput, calls=%fused_computation.8 | convolution fusion | flops 269484032 | bytes 5308416 | tf_op jit(solution)/shard_map/dot_general | solution.py:8
  96.1 4.6 %all-to-all-start.2 = ((bf16[4,32,4096]{2,1,0:T(8,128)(2,1)}), bf16[4,32,4096]{2,1,0:T(8,128)(2,1)S(1)}, u32[]{:S(2)}, u32[]{:S(2)}) async-start(bf16[4,32,4096]{2,1,0:T(8,128)(2,1)} %bitcast.9), calls=%async_computation.2 | async-start | bytes 2097152 | tf_op jit(solution)/shard_map/all_to_all | solution.py:97
  100.7 0.2 lt.48
  100.8 25.9 %all-to-all-done.2 = bf16[4,32,4096]{2,1,0:T(8,128)(2,1)S(1)} async-done(((bf16[4,32,4096]{2,1,0:T(8,128)(2,1)}), bf16[4,32,4096]{2,1,0:T(8,128)(2,1)S(1)}, u32[]{:S(2)}, u32[]{:S(2)}) %all-to-all-start.2) | async-done | bytes 1048608 | tf_op jit(solution)/shard_map/all_to_all | solution.py:97
  126.8 2.2 %gather_fusion.3 = bf16[128,4096]{1,0:T(8,128)(2,1)} fusion(bf16[128,4096]{1,0:T(8,128)(2,1)S(1)} %bitcast.47, s32[1024]{0:T(1024)S(1)} %pad_clamp_fusion), kind=kCustom, calls=%fused_computation.3 | custom fusion | bytes 2097664 | tf_op jit(solution)/shard_map/gather | solution.py:105
  128.9 2.4 %reshape.121 = f32[64,2,4096]{2,1,0:T(2,128)S(1)} reshape(bf16[128,4096]{1,0:T(8,128)(2,1)} %gather_fusion.3) | data formatting | bytes 3145728 | tf_op jit(solution)/shard_map/convert_element_type | solution.py:105
  131.3 4.8 %select_reduce_fusion = bf16[64,4096]{1,0:T(8,128)(2,1)} fusion(f32[64,2,4096]{2,1,0:T(2,128)S(1)} %reshape.121, pred[64,2]{1,0:T(8,128)(4,1)S(1)} %lt.48), kind=kLoop, calls=%fused_computation.20 | loop fusion | flops 786432 | bytes 2621568 | tf_op jit(solution)/shard_map/reduce_sum | solution.py:107
  136.1 0.0 reduce-scatter.3.cloned.1.call-done
  136.1 2.2 %slice_bitcast_fusion = (bf16[1,1024,256]{2,1,0:T(8,128)(2,1)}, bf16[1,1024,256]{2,1,0:T(8,128)(2,1)}) fusion(bf16[1024,512]{1,0:T(8,128)(2,1)} %reduce-scatter.3.cloned.1.call-done), kind=kLoop, calls=%fused_computation.23 | loop fusion | bytes 2097152 | tf_op jit(solution)/shard_map/broadcast_in_dim | solution.py:111
  138.4 29.5 %reduce-scatter.5.cloned.1.call-done = bf16[64,4096]{1,0:T(8,128)(2,1)} async-done(((bf16[256,4096]{1,0:T(8,128)(2,1)}), bf16[64,4096]{1,0:T(8,128)(2,1)}) %reduce-scatter.5.cloned.1.call-update) | async-done | bytes 524304 | tf_op jit(solution)/shard_map/reduce_scatter | solution.py:88
  (7 shorter events, 0.0 us)
Async XLA Ops:
  7.2 7.1 %copy-start = (bf16[64,4096]{1,0:T(8,128)(2,1)S(1)}, bf16[64,4096]{1,0:T(8,128)(2,1)}, u32[]{:S(2)}) copy-start(bf16[64,4096]{1,0:T(8,128)(2,1)} %param.8) | copy-start | bytes 1572868
  7.2 47.1 %all-gather.11.cloned.1.call-start = ((), (), s32[]{:S(2)}) async-start(), calls=%async_computation.9 | async-start | bytes 2621440 | tf_op jit(solution)/shard_map/all_gather | solution.py:65
  7.9 51.1 %all-gather.9.cloned.1.call-start = ((), (), s32[]{:S(2)}) async-start(), calls=%async_computation.8 | async-start | bytes 2621440 | tf_op jit(solution)/shard_map/all_gather | solution.py:66
  14.3 1.2 copy-start.1
  18.6 32.1 %all-to-all-start.1 = ((bf16[4,32,4096]{2,1,0:T(8,128)(2,1)}), bf16[4,32,4096]{2,1,0:T(8,128)(2,1)S(1)}, u32[]{:S(2)}, u32[]{:S(2)}) async-start(bf16[4,32,4096]{2,1,0:T(8,128)(2,1)} %get-tuple-element.11), calls=%async_computation.1 | async-start | bytes 2097152 | tf_op jit(solution)/shard_map/all_to_all | solution.py:43
  25.0 58.3 %all-gather.7.cloned.1.call-start = ((), (), s32[]{:S(2)}) async-start(), calls=%async_computation.7 | async-start | bytes 2621440 | tf_op jit(solution)/shard_map/all_gather | solution.py:67
  50.7 28.8 %all-to-all-start = ((bf16[4,32,4096]{2,1,0:T(8,128)(2,1)}), bf16[4,32,4096]{2,1,0:T(8,128)(2,1)S(1)}, u32[]{:S(2)}, u32[]{:S(2)}) async-start(bf16[4,32,4096]{2,1,0:T(8,128)(2,1)} %get-tuple-element.10), calls=%async_computation | async-start | bytes 2097152 | tf_op jit(solution)/shard_map/all_to_all | solution.py:50
  54.2 81.9 %reduce-scatter.3.cloned.1.call-start = ((), (), s32[]{:S(2)}) async-start(), calls=%async_computation.5 | async-start | bytes 5242880 | tf_op jit(solution)/shard_map/reduce_scatter | solution.py:81
  88.9 78.9 %reduce-scatter.5.cloned.1.call-start = ((), (), s32[]{:S(2)}) async-start(), calls=%async_computation.6 | async-start | bytes 2621440 | tf_op jit(solution)/shard_map/reduce_scatter | solution.py:88
  91.1 1.6 copy-start.2
  92.7 1.6 copy-start.3
  96.1 30.7 %all-to-all-start.2 = ((bf16[4,32,4096]{2,1,0:T(8,128)(2,1)}), bf16[4,32,4096]{2,1,0:T(8,128)(2,1)S(1)}, u32[]{:S(2)}, u32[]{:S(2)}) async-start(bf16[4,32,4096]{2,1,0:T(8,128)(2,1)} %bitcast.9), calls=%async_computation.2 | async-start | bytes 2097152 | tf_op jit(solution)/shard_map/all_to_all | solution.py:97
Sparse Core Ops, SparseCore 0:
  9.5 25.2 all-gather.10
  36.4 22.5 all-gather.8
  60.6 22.5 all-gather.6
  89.0 44.6 reduce-scatter.2
  136.6 31.1 reduce-scatter.4
where the time goes:
time: 175 us; the launch traced here: 174 us
  waiting for transfers between devices  107 us (61%)
  local copies, waits for them, and re-layouts  16.1 us (9%)
  starting transfers between devices  14.6 us (8%)
  matrix products  14.4 us (8%)
  between operations  13.9 us (8%)
  other arithmetic  7.88 us (5%)
    reduce_scatter x1, waiting for transfers between devices, local(): lax.psum_scatter(contract_first(columns, cot_in).astype(jnp.bfloat16), 't...  29.5 us
    all_to_all x1, waiting for transfers between devices, local(): lax.all_to_all(rows_out.reshape(experts, capacity, model_width), 'expert'...  25.9 us
    all_to_all x1, waiting for transfers between devices, local(): lax.all_to_all(send_rows.reshape(experts, capacity, model_width), 'expert...  25 us
    all_to_all x1, waiting for transfers between devices, local(): lax.all_to_all(send_cot.reshape(experts, capacity, model_width), 'expert'...  18.4 us
    all_to_all x1, starting transfers between devices, local(): lax.all_to_all(send_rows.reshape(experts, capacity, model_width), 'expert...  6.35 us
    dot_general x2, matrix products, contract_first(): lax.dot_general(left, right, (((0,), (0,)), ((), ())), preferred_element_...  5.35 us
    dot_general x3, matrix products, contract_last(): lax.dot_general(left, right, (((1,), (1,)), ((), ())), preferred_element_...  5.03 us
    reduce_sum x1, other arithmetic, local(): jnp.sum(gathered.reshape(tok_rows, 2, model_width), axis=1)  4.83 us
  transfers between devices with their start and end apart: 8, of which 6 were waited for; matrix products, arithmetic and copies ran while one was open for 17% of the time, Pallas kernels for 0%

commit v1 on v0

--- a/solution.py
+++ b/solution.py
@@ -1,7 +1,13 @@
 import jax
 import jax.numpy as jnp
 from jax import lax
+from jax.experimental import pallas as pl
+from jax.experimental.pallas import tpu as pltpu
 from jax.sharding import PartitionSpec as P
+
+MESH = pl.DeviceIdType.MESH
+SEND_ORDER = (2, 3, 1, 0)
+WORK_ORDER = (2, 1, 0, 3)
 
 
 def contract_last(left, right):
@@ -16,7 +22,255 @@
     )
 
 
-def local(tokens, cotangent, expert_ids, gate_wts, w_gate, w_up, w_down):
+def dot(left, right):
+    return jnp.dot(left, right, preferred_element_type=jnp.float32)
+
+
+def flip(index, mask):
+    out = index
+    for bit in (1, 2):
+        if mask & bit:
+            out = out + bit - 2 * bit * ((index // bit) % 2)
+    return out
+
+
+def kernel(
+    tok, cot, ids, gat, wg, wu, wd,
+    ig, gg, gu, gd,
+    srow, scot, rrow, rcot, wdf, part, par, pbs, pbr, act, rets, retr, gds, gdr,
+    d_ss, d_rs, w_ss, w_rs, a_ss, a_rs, b_ss, b_rs, c_ss, c_rs, r_ss, r_rs, g_ss, g_rs, l_s,
+):
+    n_exp, n_ten = 4, 4
+    toks, width = tok.shape
+    cols = width // n_ten
+    cap = srow.shape[1]
+    half = n_ten * cap // 2
+    ff_t = wd.shape[1]
+    g = lax.axis_index("group")
+    e = lax.axis_index("expert")
+    t = lax.axis_index("tensor")
+    ex = [flip(e, r) for r in range(n_exp)]
+    tx = [flip(t, q) for q in range(n_ten)]
+
+    def dcol(q):
+        return pl.ds(pl.multiple_of(tx[q] * cols, cols), cols)
+
+    def drow(q):
+        return pl.ds(pl.multiple_of(tx[q] * cap, cap), cap)
+
+    def dff(q):
+        return pl.ds(pl.multiple_of(tx[q] * ff_t, ff_t), ff_t)
+
+    sends = []
+
+    def remote(src, dst, ss, rs, r, q):
+        c = pltpu.make_async_remote_copy(
+            src_ref=src, dst_ref=dst, send_sem=ss, recv_sem=rs,
+            device_id=(g, ex[r], tx[q]), device_id_type=MESH,
+        )
+        c.start()
+        sends.append(c)
+        return c
+
+    def move(src, dst, sem):
+        c = pltpu.make_async_copy(src, dst, sem)
+        c.start()
+        return c
+
+    barrier = pltpu.get_barrier_semaphore()
+    for r in range(n_exp):
+        for q in range(n_ten):
+            if r or q:
+                pl.semaphore_signal(
+                    barrier, inc=1, device_id=(g, ex[r], tx[q]), device_id_type=MESH
+                )
+
+    id0, id1 = ids[0:1, :], ids[1:2, :]
+    lab = lax.broadcasted_iota(jnp.int32, (8, toks), 0)
+    oh0 = (jnp.broadcast_to(id0, (8, toks)) == lab).astype(jnp.float32)
+    oh1 = (jnp.broadcast_to(id1, (8, toks)) == lab).astype(jnp.float32)
+    before = (
+        lax.broadcasted_iota(jnp.int32, (toks, toks), 0)
+        < lax.broadcasted_iota(jnp.int32, (toks, toks), 1)
+    ).astype(jnp.bfloat16)
+    count = dot((oh0 + oh1).astype(jnp.bfloat16), before)
+    p0 = jnp.sum(oh0 * count, axis=0, keepdims=True)
+    p1 = jnp.sum(oh1 * (count + oh0), axis=0, keepdims=True)
+    none = -1.0
+    s0 = jnp.where(p0 < cap, id0.astype(jnp.float32) * cap + p0, none)
+    s1 = jnp.where(p1 < cap, id1.astype(jnp.float32) * cap + p1, none)
+    gate0, gate1 = gat[0:1, :], gat[1:2, :]
+
+    def place(r):
+        slot = (ex[r] * cap + lax.broadcasted_iota(jnp.int32, (cap, toks), 0)).astype(jnp.float32)
+        return slot == jnp.broadcast_to(s0, (cap, toks)), slot == jnp.broadcast_to(s1, (cap, toks))
+
+    disp, wcp, locs = {}, {}, {}
+    picks = {}
+    first = True
+    for r in SEND_ORDER:
+        m0, m1 = place(r)
+        pick = (m0 | m1).astype(jnp.bfloat16)
+        picks[r] = pick
+        scale = jnp.sum(
+            jnp.where(m0, jnp.broadcast_to(gate0, m0.shape), 0.0)
+            + jnp.where(m1, jnp.broadcast_to(gate1, m1.shape), 0.0),
+            axis=1, keepdims=True,
+        )
+        srow[r] = dot(pick, tok[...]).astype(jnp.bfloat16)
+        scot[r] = (scale * dot(pick, cot[...])).astype(jnp.bfloat16)
+        if first:
+            pl.semaphore_wait(barrier, n_exp * n_ten - 1)
+            first = False
+        for q in (3, 2, 1, 0):
+            for k, (sb, rb) in enumerate(((srow, rrow), (scot, rcot))):
+                src = sb.at[r, :, dcol(q)]
+                dst = rb.at[r, drow(0), :]
+                if r or q:
+                    disp[k, r, q] = remote(src, dst, d_ss.at[k, r, q], d_rs.at[k, r, q], r, q)
+                else:
+                    locs["d", k] = move(src, dst, l_s.at[k])
+        if r == SEND_ORDER[0]:
+            for q in (3, 2, 1, 0):
+                src = wd.at[0, :, dcol(q)]
+                dst = wdf.at[dff(0), :]
+                if q:
+                    wcp[q] = remote(src, dst, w_ss.at[q], w_rs.at[q], 0, q)
+                else:
+                    locs["w"] = move(src, dst, l_s.at[2])
+
+    odd = t % 2
+    mine = pl.ds(pl.multiple_of(odd * half, half), half)
+    other = pl.ds(pl.multiple_of((1 - odd) * half, half), half)
+
+    rcp = {}
+    for pos, r in enumerate(WORK_ORDER):
+        for q in range(n_ten):
+            for k in range(2):
+                if r or q:
+                    disp[k, r, q].wait_recv()
+                else:
+                    locs["d", k].wait()
+        if pos == 0:
+            locs["w"].wait()
+            for q in range(1, n_ten):
+                wcp[q].wait_recv()
+        x = rrow[r]
+        part[r, 0] = dot(x, wg[0])
+        part[r, 1] = dot(x, wu[0])
+        part[r, 2] = contract_last(rcot[r], wdf[...])
+        a = remote(part.at[r, :, other, :], par.at[r], a_ss.at[r], a_rs.at[r], 0, 1)
+        a.wait_recv()
+        total = part[r, :, mine, :] + par[r]
+        pbs[r] = total.astype(jnp.bfloat16)
+        b = remote(pbs.at[r], pbr.at[r], b_ss.at[r], b_rs.at[r], 0, 2)
+        b.wait_recv()
+        total = total + pbr[r].astype(jnp.float32)
+        pre_gate, pre_up, grad_hidden = total[0], total[1], total[2]
+        sig = jax.nn.sigmoid(pre_gate)
+        silu = pre_gate * sig
+        act[r, 0, mine, :] = (silu * pre_up).astype(jnp.bfloat16)
+        act[r, 1, mine, :] = (
+            grad_hidden * pre_up * sig * (1.0 + pre_gate * (1.0 - sig))
+        ).astype(jnp.bfloat16)
+        act[r, 2, mine, :] = (grad_hidden * silu).astype(jnp.bfloat16)
+        c = remote(act.at[r, :, mine, :], act.at[r, :, mine, :], c_ss.at[r], c_rs.at[r], 0, 1)
+        c.wait_recv()
+        rets[r] = (contract_last(act[r, 1], wg[0]) + contract_last(act[r, 2], wu[0])).astype(
+            jnp.bfloat16
+        )
+        for q in (3, 2, 1, 0):
+            src = rets.at[r, drow(q), :]
+            dst = retr.at[r, :, dcol(0)]
+            if r or q:
+                rcp[r, q] = remote(src, dst, r_ss.at[r, q], r_rs.at[r, q], r, q)
+            else:
+                locs["r"] = move(src, dst, l_s.at[3])
+
+    slots = n_exp * n_ten * cap
+    wide = act.shape[3]
+    cot_all = rcot[...].reshape(slots, cols)
+    hid = act[:, 0].reshape(slots, wide)
+    gds[...] = contract_first(hid, cot_all).astype(jnp.bfloat16)
+    gcp = {}
+    for q in (3, 2, 1, 0):
+        src = gds.at[dff(q), :]
+        dst = gdr.at[:, dcol(0)]
+        if q:
+            gcp[q] = remote(src, dst, g_ss.at[q], g_rs.at[q], 0, q)
+        else:
+            locs["g"] = move(src, dst, l_s.at[4])
+    rows_all = rrow[...].reshape(slots, cols)
+    gg[0] = contract_first(rows_all, act[:, 1].reshape(slots, wide)).astype(jnp.bfloat16)
+    gu[0] = contract_first(rows_all, act[:, 2].reshape(slots, wide)).astype(jnp.bfloat16)
+
+    locs["g"].wait()
+    for q in range(1, n_ten):
+        gcp[q].wait_recv()
+    gd[0] = gdr[...]
+    locs["r"].wait()
+    for r in range(n_exp):
+        for q in range(n_ten):
+            if r or q:
+                rcp[r, q].wait_recv()
+    pick = jnp.concatenate([picks[r] for r in range(n_exp)], axis=0)
+    ig[...] = contract_first(pick, retr[...].reshape(n_exp * cap, width)).astype(jnp.bfloat16)
+    for c in sends:
+        c.wait_send()
+
+
+def fused(tokens, cotangent, expert_ids, gate_wts, w_gate, w_up, w_down):
+    toks, width = tokens.shape
+    n = 4
+    cap = 2 * toks // n
+    cols = w_gate.shape[1]
+    wide = w_gate.shape[2]
+    half = n * cap // 2
+    bf, f32 = jnp.bfloat16, jnp.float32
+    dma = pltpu.SemaphoreType.DMA
+    vmem = pl.BlockSpec(memory_space=pltpu.VMEM)
+    return pl.pallas_call(
+        kernel,
+        out_shape=(
+            jax.ShapeDtypeStruct(tokens.shape, bf),
+            jax.ShapeDtypeStruct(w_gate.shape, bf),
+            jax.ShapeDtypeStruct(w_up.shape, bf),
+            jax.ShapeDtypeStruct(w_down.shape, bf),
+        ),
+        in_specs=[vmem] * 7,
+        out_specs=(vmem,) * 4,
+        scratch_shapes=[
+            pltpu.VMEM((n, cap, width), bf),
+            pltpu.VMEM((n, cap, width), bf),
+            pltpu.VMEM((n, n * cap, cols), bf),
+            pltpu.VMEM((n, n * cap, cols), bf),
+            pltpu.VMEM((wide, cols), bf),
+            pltpu.VMEM((n, 3, n * cap, wide), f32),
+            pltpu.VMEM((n, 3, half, wide), f32),
+            pltpu.VMEM((n, 3, half, wide), bf),
+            pltpu.VMEM((n, 3, half, wide), bf),
+            pltpu.VMEM((n, 3, n * cap, wide), bf),
+            pltpu.VMEM((n, n * cap, cols), bf),
+            pltpu.VMEM((n, cap, width), bf),
+            pltpu.VMEM((wide, cols), bf),
+            pltpu.VMEM(w_down.shape[1:], bf),
+            dma((2, n, n)), dma((2, n, n)),
+            dma((n,)), dma((n,)),
+            dma((n,)), dma((n,)),
+            dma((n,)), dma((n,)),
+            dma((n,)), dma((n,)),
+            dma((n, n)), dma((n, n)),
+            dma((n,)), dma((n,)),
+            dma((5,)),
+        ],
+        compiler_params=pltpu.CompilerParams(
+            collective_id=0, has_side_effects=True, vmem_limit_bytes=48 * 1024 * 1024
+        ),
+        name="expert_backward",
+    )(tokens, cotangent, expert_ids.T, gate_wts.T, w_gate, w_up, w_down)
+
+
+def plain(tokens, cotangent, expert_ids, gate_wts, w_gate, w_up, w_down):
     tok_rows, model_width = tokens.shape
     experts = lax.axis_size("expert")
     capacity = 2 * tok_rows // experts
@@ -114,6 +368,14 @@
 
 
 def solution(mesh):
+    n_exp, n_ten = mesh.shape["expert"], mesh.shape["tensor"]
+
+    def local(tokens, cotangent, expert_ids, gate_wts, w_gate, w_up, w_down):
+        args = (tokens, cotangent, expert_ids, gate_wts, w_gate, w_up, w_down)
+        capacity = 2 * tokens.shape[0] // n_exp
+        small = n_exp == 4 and n_ten == 4 and capacity % 16 == 0
+        return fused(*args) if small else plain(*args)
+
     return jax.shard_map(
         local,
         mesh=mesh,

time: 175 us -> 97.7 us (0.56)
  waiting for transfers between devices: 107 us -> 0 us
  Pallas kernels: 0 us -> 87.6 us
  starting transfers between devices: 14.6 us -> 0 us
  matrix products: 14.4 us -> 0 us
  between operations: 13.9 us -> 0.66 us
  other arithmetic: 7.88 us -> 0 us
  local copies, waits for them, and re-layouts: 16.1 us -> 9.06 us
    pallas_call x0 -> x1, Pallas kernels: none -> 87.6 us  [fused(): pl.pallas_call(kernel, out_shape=(jax.ShapeDtypeStruct(tokens.shape, bf),...]
    all_to_all x3 -> x0, waiting for transfers between devices: 69.3 us -> none  [the longest x1 25.9 us: local(): lax.all_to_all(rows_out.reshape(experts, capacity, model_width), 'expert'...]
    reduce_scatter x2 -> x0, waiting for transfers between devices: 29.5 us -> none  [the longest x1 29.5 us: local(): lax.psum_scatter(contract_first(columns, cot_in).astype(jnp.bfloat16), 't...]
    all_to_all x3 -> x0, starting transfers between devices: 14.5 us -> none  [the longest x1 6.35 us: local(): lax.all_to_all(send_rows.reshape(experts, capacity, model_width), 'expert...]
    dot_general x7 -> x0, matrix products: 14.4 us -> none  [the longest x2 5.35 us: contract_first(): lax.dot_general(left, right, (((0,), (0,)), ((), ())), preferred_element_...]
    all_gather x3 -> x0, waiting for transfers between devices: 6.45 us -> none  [the longest x1 3.75 us: local(): lax.all_gather(down_shard, 'tensor', axis=0, tiled=True)]
    gather x4 -> x0, local copies, waits for them, and re-layouts: 5.78 us -> none  [the longest x1 2.17 us: local(): gathered = returned[jnp.minimum(target, slots_all - 1)].astype(jnp.float32)]
    unnamed x10 -> x18, local copies, waits for them, and re-layouts: 3.9 us -> 9.06 us
  transfers between devices with their start and end apart: 8 -> 0, of which waited for: 6 -> 0; matrix products, arithmetic and copies ran while one was open for 17% -> 0% of each run, Pallas kernels for 0% -> 0%
where the time goes in v1:
time: 97.7 us; the launch traced here: 97.3 us
  Pallas kernels  87.6 us (90%)
  local copies, waits for them, and re-layouts  9.06 us (9%)
    pallas_call x1, Pallas kernels, fused(): pl.pallas_call(kernel, out_shape=(jax.ShapeDtypeStruct(tokens.shape, bf),...  87.6 us
    unnamed x18, local copies, waits for them, and re-layouts  9.06 us

profile of v1, /device:TPU:0, one launch (start us, length us, event | category | flops | bytes accessed | tf_op | source)
XLA Modules:
  0.0 97.3 jit_solution(3724872845430952877)
XLA Ops:
  0.6 0.0 copy-start.6
  0.6 0.0 copy-start.5
  0.7 0.7 copy-done.6
  1.3 0.0 copy-done.5
  1.3 0.0 copy-start
  1.3 1.0 %copy-done = bf16[64,4096]{1,0:T(8,128)(2,1)S(1)} copy-done((bf16[64,4096]{1,0:T(8,128)(2,1)S(1)}, bf16[64,4096]{1,0:T(8,128)(2,1)}, u32[]{:S(2)}) %copy-start) | copy-done | bytes 524312
  2.4 0.0 copy-start.1
  2.4 1.0 %copy-done.1 = bf16[64,4096]{1,0:T(8,128)(2,1)S(1)} copy-done((bf16[64,4096]{1,0:T(8,128)(2,1)S(1)}, bf16[64,4096]{1,0:T(8,128)(2,1)}, u32[]{:S(2)}) %copy-start.1) | copy-done | bytes 524312
  3.4 0.0 copy-start.2
  3.4 1.0 %copy-done.2 = bf16[1,1024,256]{2,1,0:T(8,128)(2,1)S(1)} copy-done((bf16[1,1024,256]{2,1,0:T(8,128)(2,1)S(1)}, bf16[1,1024,256]{2,1,0:T(8,128)(2,1)}, u32[]{:S(2)}) %copy-start.2) | copy-done | bytes 524312
  4.5 0.0 copy-start.3
  4.5 1.0 %copy-done.3 = bf16[1,1024,256]{2,1,0:T(8,128)(2,1)S(1)} copy-done((bf16[1,1024,256]{2,1,0:T(8,128)(2,1)S(1)}, bf16[1,1024,256]{2,1,0:T(8,128)(2,1)}, u32[]{:S(2)}) %copy-start.3) | copy-done | bytes 524312
  5.5 0.0 copy-start.4
  5.5 1.0 %copy-done.4 = bf16[1,64,4096]{2,1,0:T(8,128)(2,1)S(1)} copy-done((bf16[1,64,4096]{2,1,0:T(8,128)(2,1)S(1)}, bf16[1,64,4096]{2,1,0:T(8,128)(2,1)}, u32[]{:S(2)}) %copy-start.4) | copy-done | bytes 524312
  6.5 87.6 %expert_backward.1 = (bf16[64,4096]{1,0:T(8,128)(2,1)S(1)}, bf16[1,1024,256]{2,1,0:T(8,128)(2,1)S(1)}, bf16[1,1024,256]{2,1,0:T(8,128)(2,1)S(1)}, bf16[1,64,4096]{2,1,0:T(8,128)(2,1)S(1)}) custom-call(bf16[64,4096]{1,0:T(8,128)(2,1)S(1)} %copy-done, bf16[64,4096]{1,0:T(8,128)(2,1)S(1)} %copy-done.1, s32[2,64]{1,0:T(2,128)S(1)} %bitcast.2, ...), custom_call_target="tpu_custom_call" | custom-call | tf_op jit(solution)/shard_map/expert_backward/pallas_call | solution.py:232
  94.2 0.8 copy.15
  94.9 0.8 copy.16
  95.7 0.8 copy.17
  96.5 0.8 copy.18
Async XLA Ops:
  0.6 0.7 copy-start.6
  0.6 0.7 copy-start.5
  1.3 1.0 %copy-start = (bf16[64,4096]{1,0:T(8,128)(2,1)S(1)}, bf16[64,4096]{1,0:T(8,128)(2,1)}, u32[]{:S(2)}) copy-start(bf16[64,4096]{1,0:T(8,128)(2,1)} %tok.1) | copy-start | bytes 1572868
  2.4 1.0 %copy-start.1 = (bf16[64,4096]{1,0:T(8,128)(2,1)S(1)}, bf16[64,4096]{1,0:T(8,128)(2,1)}, u32[]{:S(2)}) copy-start(bf16[64,4096]{1,0:T(8,128)(2,1)} %cot.1) | copy-start | bytes 1572868
  3.4 1.0 %copy-start.2 = (bf16[1,1024,256]{2,1,0:T(8,128)(2,1)S(1)}, bf16[1,1024,256]{2,1,0:T(8,128)(2,1)}, u32[]{:S(2)}) copy-start(bf16[1,1024,256]{2,1,0:T(8,128)(2,1)} %wg.1) | copy-start | bytes 1572868
  4.5 1.0 %copy-start.3 = (bf16[1,1024,256]{2,1,0:T(8,128)(2,1)S(1)}, bf16[1,1024,256]{2,1,0:T(8,128)(2,1)}, u32[]{:S(2)}) copy-start(bf16[1,1024,256]{2,1,0:T(8,128)(2,1)} %wu.1) | copy-start | bytes 1572868
  5.5 1.0 %copy-start.4 = (bf16[1,64,4096]{2,1,0:T(8,128)(2,1)S(1)}, bf16[1,64,4096]{2,1,0:T(8,128)(2,1)}, u32[]{:S(2)}) copy-start(bf16[1,64,4096]{2,1,0:T(8,128)(2,1)} %wd.1) | copy-start | bytes 1572868

commit v2 on v1

--- a/solution.py
+++ b/solution.py
@@ -6,8 +6,6 @@
 from jax.sharding import PartitionSpec as P
 
 MESH = pl.DeviceIdType.MESH
-SEND_ORDER = (2, 3, 1, 0)
-WORK_ORDER = (2, 1, 0, 3)
 
 
 def contract_last(left, right):
@@ -35,9 +33,9 @@
 
 
 def kernel(
-    tok, cot, ids, gat, wg, wu, wd,
+    h_tok, h_cot, ids, gat, h_wg, h_wu, h_wd,
     ig, gg, gu, gd,
-    srow, scot, rrow, rcot, wdf, part, par, pbs, pbr, act, rets, retr, gds, gdr,
+    tok, cot, wg, wu, srow, scot, rrow, rcot, wdf, part, par, pbs, pbr, act, rets, retr, gds, gdr,
     d_ss, d_rs, w_ss, w_rs, a_ss, a_rs, b_ss, b_rs, c_ss, c_rs, r_ss, r_rs, g_ss, g_rs, l_s,
 ):
     n_exp, n_ten = 4, 4
@@ -45,7 +43,7 @@
     cols = width // n_ten
     cap = srow.shape[1]
     half = n_ten * cap // 2
-    ff_t = wd.shape[1]
+    ff_t = h_wd.shape[1]
     g = lax.axis_index("group")
     e = lax.axis_index("expert")
     t = lax.axis_index("tensor")
@@ -84,6 +82,12 @@
                 pl.semaphore_signal(
                     barrier, inc=1, device_id=(g, ex[r], tx[q]), device_id_type=MESH
                 )
+
+    loads = [
+        move(hbm, vmem, l_s.at[5 + j])
+        for j, (hbm, vmem) in enumerate(((h_tok, tok), (h_cot, cot), (h_wg, wg), (h_wu, wu)))
+    ]
+    locs = {"w": move(h_wd.at[0, :, dcol(0)], wdf.at[dff(0), :], l_s.at[2])}
 
     id0, id1 = ids[0:1, :], ids[1:2, :]
     lab = lax.broadcasted_iota(jnp.int32, (8, toks), 0)
@@ -105,67 +109,62 @@
         slot = (ex[r] * cap + lax.broadcasted_iota(jnp.int32, (cap, toks), 0)).astype(jnp.float32)
         return slot == jnp.broadcast_to(s0, (cap, toks)), slot == jnp.broadcast_to(s1, (cap, toks))
 
-    disp, wcp, locs = {}, {}, {}
-    picks = {}
-    first = True
-    for r in SEND_ORDER:
-        m0, m1 = place(r)
-        pick = (m0 | m1).astype(jnp.bfloat16)
-        picks[r] = pick
+    masks = {r: place(r) for r in range(n_exp)}
+    picks = {r: (masks[r][0] | masks[r][1]).astype(jnp.bfloat16) for r in range(n_exp)}
+    disp, cp, rcp = {}, {}, {}
+
+    def gather_rows(r):
+        srow[r] = dot(picks[r], tok[...]).astype(jnp.bfloat16)
+
+    def gather_cot(r):
+        m0, m1 = masks[r]
         scale = jnp.sum(
             jnp.where(m0, jnp.broadcast_to(gate0, m0.shape), 0.0)
             + jnp.where(m1, jnp.broadcast_to(gate1, m1.shape), 0.0),
             axis=1, keepdims=True,
         )
-        srow[r] = dot(pick, tok[...]).astype(jnp.bfloat16)
-        scot[r] = (scale * dot(pick, cot[...])).astype(jnp.bfloat16)
-        if first:
-            pl.semaphore_wait(barrier, n_exp * n_ten - 1)
-            first = False
-        for q in (3, 2, 1, 0):
-            for k, (sb, rb) in enumerate(((srow, rrow), (scot, rcot))):
+        scot[r] = (scale * dot(picks[r], cot[...])).astype(jnp.bfloat16)
+
+    def dispatch(r, qs, ks=(0, 1)):
+        for q in qs:
+            for k in ks:
+                sb, rb = ((srow, rrow), (scot, rcot))[k]
                 src = sb.at[r, :, dcol(q)]
                 dst = rb.at[r, drow(0), :]
                 if r or q:
                     disp[k, r, q] = remote(src, dst, d_ss.at[k, r, q], d_rs.at[k, r, q], r, q)
                 else:
                     locs["d", k] = move(src, dst, l_s.at[k])
-        if r == SEND_ORDER[0]:
-            for q in (3, 2, 1, 0):
-                src = wd.at[0, :, dcol(q)]
-                dst = wdf.at[dff(0), :]
-                if q:
-                    wcp[q] = remote(src, dst, w_ss.at[q], w_rs.at[q], 0, q)
-                else:
-                    locs["w"] = move(src, dst, l_s.at[2])
-
-    odd = t % 2
-    mine = pl.ds(pl.multiple_of(odd * half, half), half)
-    other = pl.ds(pl.multiple_of((1 - odd) * half, half), half)
-
-    rcp = {}
-    for pos, r in enumerate(WORK_ORDER):
+
+    def arrive(r):
         for q in range(n_ten):
             for k in range(2):
                 if r or q:
                     disp[k, r, q].wait_recv()
                 else:
                     locs["d", k].wait()
-        if pos == 0:
-            locs["w"].wait()
-            for q in range(1, n_ten):
-                wcp[q].wait_recv()
+
+    odd = t % 2
+    mine = pl.ds(pl.multiple_of(odd * half, half), half)
+    other = pl.ds(pl.multiple_of((1 - odd) * half, half), half)
+
+    def partial(r):
         x = rrow[r]
         part[r, 0] = dot(x, wg[0])
         part[r, 1] = dot(x, wu[0])
         part[r, 2] = contract_last(rcot[r], wdf[...])
-        a = remote(part.at[r, :, other, :], par.at[r], a_ss.at[r], a_rs.at[r], 0, 1)
-        a.wait_recv()
+        cp["a", r] = remote(part.at[r, :, other, :], par.at[r], a_ss.at[r], a_rs.at[r], 0, 1)
+
+    def cross(r):
+        cp["a", r].wait_recv()
         total = part[r, :, mine, :] + par[r]
+        par[r] = total
         pbs[r] = total.astype(jnp.bfloat16)
-        b = remote(pbs.at[r], pbr.at[r], b_ss.at[r], b_rs.at[r], 0, 2)
-        b.wait_recv()
-        total = total + pbr[r].astype(jnp.float32)
+        cp["b", r] = remote(pbs.at[r], pbr.at[r], b_ss.at[r], b_rs.at[r], 0, 2)
+
+    def activate(r):
+        cp["b", r].wait_recv()
+        total = par[r] + pbr[r].astype(jnp.float32)
         pre_gate, pre_up, grad_hidden = total[0], total[1], total[2]
         sig = jax.nn.sigmoid(pre_gate)
         silu = pre_gate * sig
@@ -174,18 +173,82 @@
             grad_hidden * pre_up * sig * (1.0 + pre_gate * (1.0 - sig))
         ).astype(jnp.bfloat16)
         act[r, 2, mine, :] = (grad_hidden * silu).astype(jnp.bfloat16)
-        c = remote(act.at[r, :, mine, :], act.at[r, :, mine, :], c_ss.at[r], c_rs.at[r], 0, 1)
-        c.wait_recv()
+        cp["c", r] = remote(
+            act.at[r, :, mine, :], act.at[r, :, mine, :], c_ss.at[r], c_rs.at[r], 0, 1
+        )
+
+    def rows_back(r):
+        cp["c", r].wait_recv()
         rets[r] = (contract_last(act[r, 1], wg[0]) + contract_last(act[r, 2], wu[0])).astype(
             jnp.bfloat16
         )
-        for q in (3, 2, 1, 0):
+
+    def give_back(r, qs):
+        for q in qs:
             src = rets.at[r, drow(q), :]
             dst = retr.at[r, :, dcol(0)]
             if r or q:
                 rcp[r, q] = remote(src, dst, r_ss.at[r, q], r_rs.at[r, q], r, q)
             else:
                 locs["r"] = move(src, dst, l_s.at[3])
+
+    near, far = (1, 0), (3, 2)
+    loads[0].wait()
+    gather_rows(2)
+    pl.semaphore_wait(barrier, n_exp * n_ten - 1)
+    dispatch(2, near, (0,))
+    wcp = {
+        q: remote(h_wd.at[0, :, dcol(q)], wdf.at[dff(0), :], w_ss.at[q], w_rs.at[q], 0, q)
+        for q in (3, 2, 1)
+    }
+    loads[1].wait()
+    gather_cot(2)
+    dispatch(2, near, (1,))
+    gather_rows(0)
+    dispatch(0, far + near, (0,))
+    gather_cot(0)
+    dispatch(0, far + near, (1,))
+    dispatch(2, far)
+    for r in (3, 1):
+        gather_rows(r)
+        gather_cot(r)
+    arrive(0)
+    loads[2].wait()
+    loads[3].wait()
+    locs["w"].wait()
+    for q in range(1, n_ten):
+        wcp[q].wait_recv()
+    partial(0)
+
+    arrive(2)
+    dispatch(3, near)
+    partial(2)
+    cross(2)
+    cross(0)
+    dispatch(1, far)
+    dispatch(3, far)
+    dispatch(1, near)
+    activate(2)
+    activate(0)
+    rows_back(2)
+    rows_back(0)
+    give_back(0, near)
+
+    arrive(3)
+    give_back(2, near)
+    partial(3)
+    arrive(1)
+    partial(1)
+    cross(3)
+    cross(1)
+    give_back(2, far)
+    give_back(0, far)
+    activate(3)
+    activate(1)
+    rows_back(3)
+    give_back(3, near)
+    rows_back(1)
+    give_back(1, far + near)
 
     slots = n_exp * n_ten * cap
     wide = act.shape[3]
@@ -200,6 +263,7 @@
             gcp[q] = remote(src, dst, g_ss.at[q], g_rs.at[q], 0, q)
         else:
             locs["g"] = move(src, dst, l_s.at[4])
+    give_back(3, far)
     rows_all = rrow[...].reshape(slots, cols)
     gg[0] = contract_first(rows_all, act[:, 1].reshape(slots, wide)).astype(jnp.bfloat16)
     gu[0] = contract_first(rows_all, act[:, 2].reshape(slots, wide)).astype(jnp.bfloat16)
@@ -229,6 +293,7 @@
     bf, f32 = jnp.bfloat16, jnp.float32
     dma = pltpu.SemaphoreType.DMA
     vmem = pl.BlockSpec(memory_space=pltpu.VMEM)
+    hbm = pl.BlockSpec(memory_space=pltpu.HBM)
     return pl.pallas_call(
         kernel,
         out_shape=(
@@ -237,9 +302,13 @@
             jax.ShapeDtypeStruct(w_up.shape, bf),
             jax.ShapeDtypeStruct(w_down.shape, bf),
         ),
-        in_specs=[vmem] * 7,
+        in_specs=[hbm, hbm, vmem, vmem, hbm, hbm, hbm],
         out_specs=(vmem,) * 4,
         scratch_shapes=[
+            pltpu.VMEM(tokens.shape, bf),
+            pltpu.VMEM(tokens.shape, bf),
+            pltpu.VMEM(w_gate.shape, bf),
+            pltpu.VMEM(w_up.shape, bf),
             pltpu.VMEM((n, cap, width), bf),
             pltpu.VMEM((n, cap, width), bf),
             pltpu.VMEM((n, n * cap, cols), bf),
@@ -261,10 +330,10 @@
             dma((n,)), dma((n,)),
             dma((n, n)), dma((n, n)),
             dma((n,)), dma((n,)),
-            dma((5,)),
+            dma((9,)),
         ],
         compiler_params=pltpu.CompilerParams(
-            collective_id=0, has_side_effects=True, vmem_limit_bytes=48 * 1024 * 1024
+            collective_id=0, has_side_effects=True, vmem_limit_bytes=67043328
         ),
         name="expert_backward",
     )(tokens, cotangent, expert_ids.T, gate_wts.T, w_gate, w_up, w_down)

time: 97.7 us -> 88.1 us (0.902)
  Pallas kernels: 87.6 us -> 82 us
  local copies, waits for them, and re-layouts: 9.06 us -> 5.18 us
    pallas_call x1, Pallas kernels: 87.6 us -> 82 us  [fused(): pl.pallas_call(kernel, out_shape=(jax.ShapeDtypeStruct(tokens.shape, bf),...]
    unnamed x18 -> x10, local copies, waits for them, and re-layouts: 9.06 us -> 5.18 us
where the time goes in v2:
time: 88.1 us; the launch traced here: 87.8 us
  Pallas kernels  82 us (93%)
  local copies, waits for them, and re-layouts  5.18 us (6%)
    pallas_call x1, Pallas kernels, fused(): pl.pallas_call(kernel, out_shape=(jax.ShapeDtypeStruct(tokens.shape, bf),...  82 us
    unnamed x10, local copies, waits for them, and re-layouts  5.18 us

profile of v2, /device:TPU:0, one launch (start us, length us, event | category | flops | bytes accessed | tf_op | source)
XLA Modules:
  0.0 87.8 jit_solution(537015006721029786)
XLA Ops:
  0.6 82.0 %expert_backward.1 = (bf16[64,4096]{1,0:T(8,128)(2,1)}, bf16[1,1024,256]{2,1,0:T(8,128)(2,1)}, bf16[1,1024,256]{2,1,0:T(8,128)(2,1)}, bf16[1,64,4096]{2,1,0:T(8,128)(2,1)}) custom-call(bf16[64,4096]{1,0:T(8,128)(2,1)} %h_tok.1, bf16[64,4096]{1,0:T(8,128)(2,1)} %h_cot.1, s32[2,64]{1,0:T(2,128)} %bitcast.2, f32[2,64]{1,0:T(2,128)} %bitcast.3, ...), custom_call_target="tpu_custom_call" | custom-call | tf_op jit(solution)/shard_map/expert_backward/pallas_call | solution.py:297
  82.6 0.0 copy-start.2
  82.6 1.9 %copy.15 = bf16[64,4096]{1,0:T(8,128)(2,1)} copy(bf16[64,4096]{1,0:T(8,128)(2,1)} %get-tuple-element.8) | data formatting | bytes 1048576
  84.6 0.0 copy-done.2
  84.6 0.0 copy-start.1
  84.6 0.8 copy.16
  85.4 0.4 copy-done.1
  85.8 0.0 copy-start
  85.8 0.8 copy.17
  86.6 0.4 copy-done
  87.0 0.8 copy.18
Async XLA Ops:
  82.6 1.9 %copy-start.2 = (bf16[1,1024,256]{2,1,0:T(8,128)(2,1)S(1)}, bf16[1,1024,256]{2,1,0:T(8,128)(2,1)}, u32[]{:S(2)}) copy-start(bf16[1,1024,256]{2,1,0:T(8,128)(2,1)} %get-tuple-element.9) | copy-start | bytes 1572868
  84.6 1.2 %copy-start.1 = (bf16[1,1024,256]{2,1,0:T(8,128)(2,1)S(1)}, bf16[1,1024,256]{2,1,0:T(8,128)(2,1)}, u32[]{:S(2)}) copy-start(bf16[1,1024,256]{2,1,0:T(8,128)(2,1)} %get-tuple-element.10) | copy-start | bytes 1572868
  85.8 1.2 %copy-start = (bf16[1,64,4096]{2,1,0:T(8,128)(2,1)S(1)}, bf16[1,64,4096]{2,1,0:T(8,128)(2,1)}, u32[]{:S(2)}) copy-start(bf16[1,64,4096]{2,1,0:T(8,128)(2,1)} %get-tuple-element.11) | copy-start | bytes 1572868

commit v3 on v2

--- a/solution.py
+++ b/solution.py
@@ -209,9 +209,11 @@
     gather_cot(0)
     dispatch(0, far + near, (1,))
     dispatch(2, far)
-    for r in (3, 1):
-        gather_rows(r)
-        gather_cot(r)
+    gather_rows(1)
+    gather_cot(1)
+    dispatch(1, far)
+    gather_rows(3)
+    gather_cot(3)
     arrive(0)
     loads[2].wait()
     loads[3].wait()
@@ -223,32 +225,30 @@
     arrive(2)
     dispatch(3, near)
     partial(2)
+    dispatch(1, near)
     cross(2)
     cross(0)
-    dispatch(1, far)
     dispatch(3, far)
-    dispatch(1, near)
     activate(2)
     activate(0)
     rows_back(2)
     rows_back(0)
-    give_back(0, near)
+    give_back(0, far + near)
+    arrive(1)
+    partial(1)
+    cross(1)
 
     arrive(3)
     give_back(2, near)
     partial(3)
-    arrive(1)
-    partial(1)
     cross(3)
-    cross(1)
     give_back(2, far)
-    give_back(0, far)
+    activate(1)
     activate(3)
-    activate(1)
-    rows_back(3)
-    give_back(3, near)
     rows_back(1)
     give_back(1, far + near)
+    rows_back(3)
+    give_back(3, near + far)
 
     slots = n_exp * n_ten * cap
     wide = act.shape[3]
@@ -263,7 +263,6 @@
             gcp[q] = remote(src, dst, g_ss.at[q], g_rs.at[q], 0, q)
         else:
             locs["g"] = move(src, dst, l_s.at[4])
-    give_back(3, far)
     rows_all = rrow[...].reshape(slots, cols)
     gg[0] = contract_first(rows_all, act[:, 1].reshape(slots, wide)).astype(jnp.bfloat16)
     gu[0] = contract_first(rows_all, act[:, 2].reshape(slots, wide)).astype(jnp.bfloat16)
@@ -283,6 +282,15 @@
         c.wait_send()
 
 
+def store(*refs):
+    sems = refs[8]
+    copies = [pltpu.make_async_copy(refs[j], refs[4 + j], sems.at[j]) for j in range(4)]
+    for c in copies:
+        c.start()
+    for c in copies:
+        c.wait()
+
+
 def fused(tokens, cotangent, expert_ids, gate_wts, w_gate, w_up, w_down):
     toks, width = tokens.shape
     n = 4
@@ -294,13 +302,13 @@
     dma = pltpu.SemaphoreType.DMA
     vmem = pl.BlockSpec(memory_space=pltpu.VMEM)
     hbm = pl.BlockSpec(memory_space=pltpu.HBM)
-    return pl.pallas_call(
+    results = pl.pallas_call(
         kernel,
         out_shape=(
-            jax.ShapeDtypeStruct(tokens.shape, bf),
-            jax.ShapeDtypeStruct(w_gate.shape, bf),
-            jax.ShapeDtypeStruct(w_up.shape, bf),
-            jax.ShapeDtypeStruct(w_down.shape, bf),
+            pltpu.VMEM(tokens.shape, bf),
+            pltpu.VMEM(w_gate.shape, bf),
+            pltpu.VMEM(w_up.shape, bf),
+            pltpu.VMEM(w_down.shape, bf),
         ),
         in_specs=[hbm, hbm, vmem, vmem, hbm, hbm, hbm],
         out_specs=(vmem,) * 4,
@@ -333,10 +341,19 @@
             dma((9,)),
         ],
         compiler_params=pltpu.CompilerParams(
-            collective_id=0, has_side_effects=True, vmem_limit_bytes=67043328
+            collective_id=0, has_side_effects=True, vmem_limit_bytes=62849024
         ),
         name="expert_backward",
     )(tokens, cotangent, expert_ids.T, gate_wts.T, w_gate, w_up, w_down)
+    return pl.pallas_call(
+        store,
+        out_shape=tuple(jax.ShapeDtypeStruct(a.shape, a.dtype) for a in results),
+        in_specs=[pl.BlockSpec(memory_space=pl.ANY)] * 4,
+        out_specs=(hbm,) * 4,
+        scratch_shapes=[dma((4,))],
+        compiler_params=pltpu.CompilerParams(vmem_limit_bytes=4 * 1024 * 1024),
+        name="store_results",
+    )(*results)
 
 
 def plain(tokens, cotangent, expert_ids, gate_wts, w_gate, w_up, w_down):

time: 88.1 us -> 85.7 us (0.973)
  local copies, waits for them, and re-layouts: 5.18 us -> 0 us
  Pallas kernels: 82 us -> 84.9 us
    unnamed x10 -> x0, local copies, waits for them, and re-layouts: 5.18 us -> none
    pallas_call x1 -> x2, Pallas kernels: 82 us -> 84.9 us  [the longest x1 83.6 us: fused(): pl.pallas_call(kernel, out_shape=(pltpu.VMEM(tokens.shape, bf), pltpu.VME...]
where the time goes in v3:
time: 85.7 us; the launch traced here: 85.6 us
  Pallas kernels  84.9 us (99%)
    pallas_call x1, Pallas kernels, fused(): pl.pallas_call(kernel, out_shape=(pltpu.VMEM(tokens.shape, bf), pltpu.VME...  83.6 us

profile of v3, /device:TPU:0, one launch (start us, length us, event | category | flops | bytes accessed | tf_op | source)
XLA Modules:
  0.0 85.6 jit_solution(7876433712365357376)
XLA Ops:
  0.6 83.6 %expert_backward.1 = (bf16[64,4096]{1,0:T(8,128)(2,1)S(1)}, bf16[1,1024,256]{2,1,0:T(8,128)(2,1)S(1)}, bf16[1,1024,256]{2,1,0:T(8,128)(2,1)S(1)}, bf16[1,64,4096]{2,1,0:T(8,128)(2,1)S(1)}) custom-call(bf16[64,4096]{1,0:T(8,128)(2,1)} %h_tok.1, bf16[64,4096]{1,0:T(8,128)(2,1)} %h_cot.1, s32[2,64]{1,0:T(2,128)} %bitcast.2, f32[2,64]{1,0:T(2,128)} %bitcast.3, ...), custom_call_target="tpu_custom_call" | custom-call | tf_op jit(solution)/shard_map/expert_backward/pallas_call | solution.py:305
  84.2 1.3 %store_results.1 = (bf16[64,4096]{1,0:T(8,128)(2,1)}, bf16[1,1024,256]{2,1,0:T(8,128)(2,1)}, bf16[1,1024,256]{2,1,0:T(8,128)(2,1)}, bf16[1,64,4096]{2,1,0:T(8,128)(2,1)}) custom-call(bf16[64,4096]{1,0:T(8,128)(2,1)S(1)} %get-tuple-element.8.refs_0_, bf16[1,1024,256]{2,1,0:T(8,128)(2,1)S(1)} %get-tuple-element.9.refs_1_, ...), custom_call_target="tpu_custom_call" | custom-call | tf_op jit(solution)/shard_map/store_results/pallas_call | solution.py:348

commit v4 on v3

--- a/solution.py
+++ b/solution.py
@@ -209,11 +209,9 @@
     gather_cot(0)
     dispatch(0, far + near, (1,))
     dispatch(2, far)
-    gather_rows(1)
-    gather_cot(1)
-    dispatch(1, far)
-    gather_rows(3)
-    gather_cot(3)
+    for r in (3, 1):
+        gather_rows(r)
+        gather_cot(r)
     arrive(0)
     loads[2].wait()
     loads[3].wait()
@@ -225,30 +223,32 @@
     arrive(2)
     dispatch(3, near)
     partial(2)
-    dispatch(1, near)
     cross(2)
     cross(0)
+    dispatch(1, far)
     dispatch(3, far)
+    dispatch(1, near)
     activate(2)
     activate(0)
     rows_back(2)
     rows_back(0)
-    give_back(0, far + near)
-    arrive(1)
-    partial(1)
-    cross(1)
+    give_back(0, near)
 
     arrive(3)
     give_back(2, near)
     partial(3)
+    arrive(1)
+    partial(1)
     cross(3)
+    cross(1)
     give_back(2, far)
+    give_back(0, far)
+    activate(3)
     activate(1)
-    activate(3)
+    rows_back(3)
+    give_back(3, near)
     rows_back(1)
     give_back(1, far + near)
-    rows_back(3)
-    give_back(3, near + far)
 
     slots = n_exp * n_ten * cap
     wide = act.shape[3]
@@ -263,6 +263,7 @@
             gcp[q] = remote(src, dst, g_ss.at[q], g_rs.at[q], 0, q)
         else:
             locs["g"] = move(src, dst, l_s.at[4])
+    give_back(3, far)
     rows_all = rrow[...].reshape(slots, cols)
     gg[0] = contract_first(rows_all, act[:, 1].reshape(slots, wide)).astype(jnp.bfloat16)
     gu[0] = contract_first(rows_all, act[:, 2].reshape(slots, wide)).astype(jnp.bfloat16)

time: 85.7 us -> 82.8 us (0.966)
  Pallas kernels: 84.9 us -> 82 us
    pallas_call x1, Pallas kernels: 83.6 us -> 80.7 us  [fused(): pl.pallas_call(kernel, out_shape=(pltpu.VMEM(tokens.shape, bf), pltpu.VME...]
where the time goes in v4:
time: 82.8 us; the launch traced here: 82.7 us
  Pallas kernels  82 us (99%)
    pallas_call x1, Pallas kernels, fused(): pl.pallas_call(kernel, out_shape=(pltpu.VMEM(tokens.shape, bf), pltpu.VME...  80.7 us

profile of v4, /device:TPU:0, one launch (start us, length us, event | category | flops | bytes accessed | tf_op | source)
XLA Modules:
  0.0 82.7 jit_solution(17747225564766627870)
XLA Ops:
  0.6 80.7 %expert_backward.1 = (bf16[64,4096]{1,0:T(8,128)(2,1)S(1)}, bf16[1,1024,256]{2,1,0:T(8,128)(2,1)S(1)}, bf16[1,1024,256]{2,1,0:T(8,128)(2,1)S(1)}, bf16[1,64,4096]{2,1,0:T(8,128)(2,1)S(1)}) custom-call(bf16[64,4096]{1,0:T(8,128)(2,1)} %h_tok.1, bf16[64,4096]{1,0:T(8,128)(2,1)} %h_cot.1, s32[2,64]{1,0:T(2,128)} %bitcast.2, f32[2,64]{1,0:T(2,128)} %bitcast.3, ...), custom_call_target="tpu_custom_call" | custom-call | tf_op jit(solution)/shard_map/expert_backward/pallas_call | solution.py:306
  81.3 1.3 %store_results.1 = (bf16[64,4096]{1,0:T(8,128)(2,1)}, bf16[1,1024,256]{2,1,0:T(8,128)(2,1)}, bf16[1,1024,256]{2,1,0:T(8,128)(2,1)}, bf16[1,64,4096]{2,1,0:T(8,128)(2,1)}) custom-call(bf16[64,4096]{1,0:T(8,128)(2,1)S(1)} %get-tuple-element.8.refs_0_, bf16[1,1024,256]{2,1,0:T(8,128)(2,1)S(1)} %get-tuple-element.9.refs_1_, ...), custom_call_target="tpu_custom_call" | custom-call | tf_op jit(solution)/shard_map/store_results/pallas_call | solution.py:349
